TPU v7x, 128 devices: a whole 4x4x4 slice. The times are simulated.
128 devices in a mesh: dp: 32 (over y, z, core), mp: 4 (over x).
Axes of the slice: x: 4, y: 4, z: 4, core: 2. Of those that a mesh axis runs over, the one named last changes fastest.
Arguments:
- table: float32 [262144, 512], P('dp', 'mp'), may hold values from -6 to 6
- first_moment: float32 [262144, 512], P('dp', 'mp'), may hold values from -1.8 to 1.8
- second_moment: float32 [262144, 512], P('dp', 'mp'), may hold values from 0.01 to 1
- grads: bfloat16 [65536, 512], P('dp', 'mp'), may hold values from -108 to 108
- ids: int32 [65536], P('dp'), may hold values from 0 to 262143, as said below
Outputs:
- new_table: float32 [262144, 512], P('dp', 'mp')
- new_first: float32 [262144, 512], P('dp', 'mp')
- new_second: float32 [262144, 512], P('dp', 'mp')
Inputs may be any that keep to these rules, and one draw needn't show every extreme that they name: `ids`: the positions of one device name at most 256 positions' worth of rows of any one owner (rows k * 8192 to (k + 1) * 8192 - 1) and at most 64 distinct rows of one owner; in every draw one owner reaches both bounds on every device.
All inputs are finite; a program needn't handle non-finite values.
Results may differ from a plain program's by a relative error of at most 0.0003.
Values may be sent and summed in bfloat16 or wider, within the bound.
A program may use at most 64 MiB of HBM per device.

v0:
```python
import jax
import jax.numpy as jnp
from jax import lax
from jax.sharding import Mesh
from jax.sharding import PartitionSpec as P

DP = ("dp_0", "dp_1", "dp_2")
DP_MP = ("dp_0", "dp_1", "dp_2", "mp")
beta_first = 0.9
beta_second = 0.999
learn_rate = 0.01
decay_rate = 0.1
adam_eps = 1e-08
first_fix = 0.9999734386
second_fix = 0.0952078529


def by_axis(shard, axes):
    for axis in axes:
        shard = lax.psum(shard, axis)
    return shard


def block_size():
    return 512


def block_starts(count, step):
    return jnp.arange(0, count, step, dtype=jnp.int32)


def pack_slots(dest, local_row, values, slots, rows_dev):
    step = block_size()

    def pack_one_block(start):
        target = start + jnp.arange(step, dtype=jnp.int32)
        match = dest[None, :] == target[:, None]
        summed = jnp.dot(match.astype(jnp.bfloat16), values, preferred_element_type=jnp.float32)
        marks = jnp.min(jnp.where(match, local_row[None, :], rows_dev), axis=1)
        return (summed, marks)

    summed, marks = lax.map(pack_one_block, block_starts(slots, step))
    return (summed.reshape(slots, values.shape[1]), marks.reshape(slots))


def gather_rows(got_row, got, rows_dev):
    step = block_size()

    def gather_one_block(start):
        target = start + jnp.arange(step, dtype=jnp.int32)
        match = got_row[None, :] == target[:, None]
        return jnp.dot(
            match.astype(jnp.float32),
            got,
            precision=lax.Precision.HIGHEST,
            preferred_element_type=jnp.float32,
        )

    return lax.map(gather_one_block, block_starts(rows_dev, step)).reshape(rows_dev, got.shape[1])


def body(table, first_moment, second_moment, grads, ids):
    peers = lax.axis_size(DP)
    rows_dev = table.shape[0]
    width = table.shape[1]
    tok_dev = grads.shape[0]
    room = tok_dev // peers
    owner = ids // rows_dev
    local_row = ids - owner * rows_dev
    place = jnp.arange(tok_dev, dtype=jnp.int32)
    step = block_size()

    def first_block(start):
        here = start + jnp.arange(step, dtype=jnp.int32)
        mine = lax.dynamic_slice_in_dim(ids, start, step)
        earlier = jnp.logical_and(ids[None, :] == mine[:, None], place[None, :] < here[:, None])
        return jnp.logical_not(jnp.any(earlier, axis=1))

    leading = lax.map(first_block, block_starts(tok_dev, step)).reshape(tok_dev)

    def rank_block(start):
        mine = lax.dynamic_slice_in_dim(ids, start, step)
        mine_owner = lax.dynamic_slice_in_dim(owner, start, step)
        below = (
            leading[None, :]
            & (owner[None, :] == mine_owner[:, None])
            & (ids[None, :] < mine[:, None])
        )
        return jnp.sum(below.astype(jnp.int32), axis=1)

    rank = lax.map(rank_block, block_starts(tok_dev, step)).reshape(tok_dev)
    dest = owner * room + rank
    slots = peers * room
    sums, marker = pack_slots(dest, local_row, grads, slots, rows_dev)
    row_marks = marker.astype(jnp.float32).reshape(peers, room)
    got, got_rows = (
        lax.all_to_all(
            sums.reshape(peers, room, width), DP, split_axis=0, concat_axis=0, tiled=True
        ),
        lax.all_to_all(row_marks, DP, split_axis=0, concat_axis=0, tiled=True),
    )
    got_index = got_rows.reshape(slots).astype(jnp.int32)
    grad_rows = gather_rows(got_index, got.reshape(slots, width), rows_dev)
    local_sum = jnp.sum(grad_rows * grad_rows)
    total = by_axis(local_sum, DP_MP)
    limit = jnp.sqrt(jnp.float32(tok_dev * peers * width * lax.axis_size("mp")))
    scale = limit / jnp.maximum(jnp.sqrt(total), limit)
    clipped = scale * grad_rows
    new_first = beta_first * first_moment + (1.0 - beta_first) * clipped
    new_second = beta_second * second_moment + (1.0 - beta_second) * clipped * clipped
    first_hat = new_first / first_fix
    second_hat = new_second / second_fix
    new_table = table - learn_rate * (
        first_hat / (jnp.sqrt(second_hat) + adam_eps) + decay_rate * table
    )
    return (new_table, new_first, new_second)


def solution(mesh):
    split = Mesh(mesh.devices.reshape(4, 4, 2, mesh.shape["mp"]), ("dp_0", "dp_1", "dp_2", "mp"))
    placed = (P(DP, "mp"), P(DP, "mp"), P(DP, "mp"), P(DP, "mp"), P(DP))
    return jax.shard_map(
        body,
        mesh=split,
        in_specs=placed,
        out_specs=(P(DP, "mp"), P(DP, "mp"), P(DP, "mp")),
        check_vma=False,
    )
```

profile of v0, /device:TPU:0, one launch (start us, length us, event | category | flops | bytes accessed | tf_op | source)
XLA Modules:
  0.0 212.3 jit_solution(10993238454056998572)
XLA Ops:
  1.4 22.3 %while.46 = (s32[]{:T(128)}, pred[4,512]{1,0:T(4,128)(4,1)S(1)}, s32[2048]{0:T(1024)}, s32[4]{0:T(128)S(1)}, s32[]{:T(128)}, /*index=5*/s32[]{:T(128)}, s32[]{:T(128)}) while((s32[]{:T(128)}, pred[4,512]{1,0:T(4,128)(4,1)S(1)}, s32[2048]{0:T(1024)}, s32[4]{0:T(128)S(1)}, s32[]{:T(128)}, /*index=5*/s32[]{:T(128)}, s32[]{:T(128)}) %tuple.67), condition=%wide.region_2.3_spmd.clone, body=%wide.region_0.2_spmd.clone.sunk | while | flops 4194821 | bytes 22159 | solution.py:79
  4.2 0.8 dynamic_slice.38
  5.0 1.9 fusion.48
  9.8 0.8 dynamic_slice.38
  10.6 1.9 fusion.48
  15.4 0.8 dynamic_slice.38
  16.1 1.9 fusion.48
  21.7 1.9 fusion.48
  23.7 20.1 %while.43 = (s32[]{:T(128)}, s32[4,512]{1,0:T(4,128)S(1)}, pred[4,512]{1,0:T(4,128)(4,1)S(1)}, s32[2048]{0:T(1024)S(1)}, s32[4]{0:T(128)S(1)}, /*index=5*/s32[2048]{0:T(1024)}, s32[]{:T(128)}, s32[]{:T(128)}, s32[]{:T(128)}) while((s32[]{:T(128)}, s32[4,512]{1,0:T(4,128)S(1)}, pred[4,512]{1,0:T(4,128)(4,1)S(1)}, s32[2048]{0:T(1024)S(1)}, ...), condition=%wide.region_5.6_spmd, body=%wide.region_3.5_spmd.sunk | while | flops 6290949 | bytes 41119 | solution.py:91
  26.1 0.8 dynamic_slice.33
  26.8 1.8 convert_reduce_fusion.3
  31.1 0.8 dynamic_slice.33
  31.9 1.8 convert_reduce_fusion.3
  36.9 1.8 convert_reduce_fusion.3
  41.9 1.8 convert_reduce_fusion.3
  44.5 18.4 %while.44 = (s32[]{:T(128)}, f32[4,512,128]{2,1,0:T(8,128)}, s32[4,512]{1,0:T(4,128)S(1)}, s32[2048]{0:T(1024)S(1)}, s32[4]{0:T(128)S(1)}, /*index=5*/bf16[2048,...) while((s32[]{:T(128)}, f32[4,512,128]{2,1,0:T(8,128)}, s32[4,512]{1,0:T(4,128)S(1)}, ...), condition=%wide.region_8.9_spmd, body=%wide.region_6.8_spmd.sunk | while | flops 272629760 | bytes 823421 | solution.py:42
  46.6 2.5 %fusion.43 = f32[4,512,128]{2,1,0:T(8,128)} fusion(f32[4,512,128]{2,1,0:T(8,128)} %get-tuple-element.385, s32[]{:T(128)S(6)} %copy.32, bf16[2048,128]{1,0:T(8,128)(2,1)} %get-tuple-element.398, s32[2048]{0:T(1024)S(1)} %get-tuple-element.396, s32[512]{0:T(512)S(1)} %iota_add_fusion.6), kind=kOutput, calls=%fused_computation.9.clone.1 | convolution fusion | flops 269484032 | bytes 796676 | tf_op jit(solution)/shard_map/while/body/eval_jaxpr/dot_general | solution.py:38
  51.2 2.5 %fusion.43 = f32[4,512,128]{2,1,0:T(8,128)} fusion(f32[4,512,128]{2,1,0:T(8,128)} %get-tuple-element.385, s32[]{:T(128)S(6)} %copy.32, bf16[2048,128]{1,0:T(8,128)(2,1)} %get-tuple-element.398, s32[2048]{0:T(1024)S(1)} %get-tuple-element.396, s32[512]{0:T(512)S(1)} %iota_add_fusion.6), kind=kOutput, calls=%fused_computation.9.clone.1 | convolution fusion | flops 269484032 | bytes 796676 | tf_op jit(solution)/shard_map/while/body/eval_jaxpr/dot_general | solution.py:38
  55.8 2.5 %fusion.43 = f32[4,512,128]{2,1,0:T(8,128)} fusion(f32[4,512,128]{2,1,0:T(8,128)} %get-tuple-element.385, s32[]{:T(128)S(6)} %copy.32, bf16[2048,128]{1,0:T(8,128)(2,1)} %get-tuple-element.398, s32[2048]{0:T(1024)S(1)} %get-tuple-element.396, s32[512]{0:T(512)S(1)} %iota_add_fusion.6), kind=kOutput, calls=%fused_computation.9.clone.1 | convolution fusion | flops 269484032 | bytes 796676 | tf_op jit(solution)/shard_map/while/body/eval_jaxpr/dot_general | solution.py:38
  60.4 2.5 %fusion.43 = f32[4,512,128]{2,1,0:T(8,128)} fusion(f32[4,512,128]{2,1,0:T(8,128)} %get-tuple-element.385, s32[]{:T(128)S(6)} %copy.32, bf16[2048,128]{1,0:T(8,128)(2,1)} %get-tuple-element.398, s32[2048]{0:T(1024)S(1)} %get-tuple-element.396, s32[512]{0:T(512)S(1)} %iota_add_fusion.6), kind=kOutput, calls=%fused_computation.9.clone.1 | convolution fusion | flops 269484032 | bytes 796676 | tf_op jit(solution)/shard_map/while/body/eval_jaxpr/dot_general | solution.py:38
  63.0 15.6 %all_to_all.11 = f32[32,1,64]{2,1,0:T(1,128)S(1)} all-to-all(f32[32,1,64]{2,1,0:T(1,128)S(1)} %convert_element_type.26), channel_id=1, replica_groups=mesh['dp_0'=4,'dp_1'=4,'dp_2'=2,'mp'=4] {'dp_0','dp_1','dp_2'}, dimensions={0} | all-to-all | bytes 16384 | tf_op jit(solution)/shard_map/all_to_all | solution.py:100
  78.7 3.9 %all-to-all-start.1 = ((f32[32,64,128]{2,1,0:T(8,128)}), f32[32,64,128]{2,1,0:T(8,128)S(1)}, u32[]{:S(2)}, u32[]{:S(2)}) async-start(f32[32,64,128]{2,1,0:T(8,128)} %bitcast.7), calls=%async_computation.1 | async-start | bytes 2097152 | tf_op jit(solution)/shard_map/all_to_all | solution.py:97
  82.8 16.6 %all-to-all-done.1 = f32[32,64,128]{2,1,0:T(8,128)S(1)} async-done(((f32[32,64,128]{2,1,0:T(8,128)}), f32[32,64,128]{2,1,0:T(8,128)S(1)}, u32[]{:S(2)}, u32[]{:S(2)}) %all-to-all-start.1) | async-done | bytes 1048608 | tf_op jit(solution)/shard_map/all_to_all | solution.py:97
  99.4 62.8 %while.45 = (s32[]{:T(128)}, f32[16,512,128]{2,1,0:T(8,128)}, s32[2048]{0:T(1024)S(1)}, s32[16]{0:T(128)S(1)}, f32[2048,128]{1,0:T(8,128)S(1)}, /*index=5*/s32[]{:T(128)}) while((s32[]{:T(128)}, f32[16,512,128]{2,1,0:T(8,128)}, s32[2048]{0:T(1024)S(1)}, s32[16]{0:T(128)S(1)}, f32[2048,128]{1,0:T(8,128)S(1)}, /*index=5*/s32[]{:T(128)}) %tuple.79), condition=%wide.region_10.11_spmd, body=%wide.region_9.10_spmd.sunk | while | flops 1611661824 | bytes 1323105 | solution.py:59
  100.6 2.7 %fusion.47 = f32[16,512,128]{2,1,0:T(8,128)} fusion(f32[16,512,128]{2,1,0:T(8,128)} %get-tuple-element.409, s32[]{:T(128)S(6)} %copy.40, f32[2048,128]{1,0:T(8,128)S(1)} %get-tuple-element.418, s32[2048]{0:T(1024)S(1)} %get-tuple-element.416, s32[512]{0:T(512)S(1)} %iota_add_fusion.7), kind=kOutput, calls=%fused_computation.16.clone.1 | convolution fusion | flops 1611661312 | bytes 1320964 | tf_op jit(solution)/shard_map/while/body/eval_jaxpr/dot_general | solution.py:52
  104.5 2.7 %fusion.47 = f32[16,512,128]{2,1,0:T(8,128)} fusion(f32[16,512,128]{2,1,0:T(8,128)} %get-tuple-element.409, s32[]{:T(128)S(6)} %copy.40, f32[2048,128]{1,0:T(8,128)S(1)} %get-tuple-element.418, s32[2048]{0:T(1024)S(1)} %get-tuple-element.416, s32[512]{0:T(512)S(1)} %iota_add_fusion.7), kind=kOutput, calls=%fused_computation.16.clone.1 | convolution fusion | flops 1611661312 | bytes 1320964 | tf_op jit(solution)/shard_map/while/body/eval_jaxpr/dot_general | solution.py:52
  108.5 2.7 %fusion.47 = f32[16,512,128]{2,1,0:T(8,128)} fusion(f32[16,512,128]{2,1,0:T(8,128)} %get-tuple-element.409, s32[]{:T(128)S(6)} %copy.40, f32[2048,128]{1,0:T(8,128)S(1)} %get-tuple-element.418, s32[2048]{0:T(1024)S(1)} %get-tuple-element.416, s32[512]{0:T(512)S(1)} %iota_add_fusion.7), kind=kOutput, calls=%fused_computation.16.clone.1 | convolution fusion | flops 1611661312 | bytes 1320964 | tf_op jit(solution)/shard_map/while/body/eval_jaxpr/dot_general | solution.py:52
  112.4 2.7 %fusion.47 = f32[16,512,128]{2,1,0:T(8,128)} fusion(f32[16,512,128]{2,1,0:T(8,128)} %get-tuple-element.409, s32[]{:T(128)S(6)} %copy.40, f32[2048,128]{1,0:T(8,128)S(1)} %get-tuple-element.418, s32[2048]{0:T(1024)S(1)} %get-tuple-element.416, s32[512]{0:T(512)S(1)} %iota_add_fusion.7), kind=kOutput, calls=%fused_computation.16.clone.1 | convolution fusion | flops 1611661312 | bytes 1320964 | tf_op jit(solution)/shard_map/while/body/eval_jaxpr/dot_general | solution.py:52
  116.3 2.7 %fusion.47 = f32[16,512,128]{2,1,0:T(8,128)} fusion(f32[16,512,128]{2,1,0:T(8,128)} %get-tuple-element.409, s32[]{:T(128)S(6)} %copy.40, f32[2048,128]{1,0:T(8,128)S(1)} %get-tuple-element.418, s32[2048]{0:T(1024)S(1)} %get-tuple-element.416, s32[512]{0:T(512)S(1)} %iota_add_fusion.7), kind=kOutput, calls=%fused_computation.16.clone.1 | convolution fusion | flops 1611661312 | bytes 1320964 | tf_op jit(solution)/shard_map/while/body/eval_jaxpr/dot_general | solution.py:52
  120.2 2.7 %fusion.47 = f32[16,512,128]{2,1,0:T(8,128)} fusion(f32[16,512,128]{2,1,0:T(8,128)} %get-tuple-element.409, s32[]{:T(128)S(6)} %copy.40, f32[2048,128]{1,0:T(8,128)S(1)} %get-tuple-element.418, s32[2048]{0:T(1024)S(1)} %get-tuple-element.416, s32[512]{0:T(512)S(1)} %iota_add_fusion.7), kind=kOutput, calls=%fused_computation.16.clone.1 | convolution fusion | flops 1611661312 | bytes 1320964 | tf_op jit(solution)/shard_map/while/body/eval_jaxpr/dot_general | solution.py:52
  124.2 2.7 %fusion.47 = f32[16,512,128]{2,1,0:T(8,128)} fusion(f32[16,512,128]{2,1,0:T(8,128)} %get-tuple-element.409, s32[]{:T(128)S(6)} %copy.40, f32[2048,128]{1,0:T(8,128)S(1)} %get-tuple-element.418, s32[2048]{0:T(1024)S(1)} %get-tuple-element.416, s32[512]{0:T(512)S(1)} %iota_add_fusion.7), kind=kOutput, calls=%fused_computation.16.clone.1 | convolution fusion | flops 1611661312 | bytes 1320964 | tf_op jit(solution)/shard_map/while/body/eval_jaxpr/dot_general | solution.py:52
  128.1 2.7 %fusion.47 = f32[16,512,128]{2,1,0:T(8,128)} fusion(f32[16,512,128]{2,1,0:T(8,128)} %get-tuple-element.409, s32[]{:T(128)S(6)} %copy.40, f32[2048,128]{1,0:T(8,128)S(1)} %get-tuple-element.418, s32[2048]{0:T(1024)S(1)} %get-tuple-element.416, s32[512]{0:T(512)S(1)} %iota_add_fusion.7), kind=kOutput, calls=%fused_computation.16.clone.1 | convolution fusion | flops 1611661312 | bytes 1320964 | tf_op jit(solution)/shard_map/while/body/eval_jaxpr/dot_general | solution.py:52
  132.0 2.7 %fusion.47 = f32[16,512,128]{2,1,0:T(8,128)} fusion(f32[16,512,128]{2,1,0:T(8,128)} %get-tuple-element.409, s32[]{:T(128)S(6)} %copy.40, f32[2048,128]{1,0:T(8,128)S(1)} %get-tuple-element.418, s32[2048]{0:T(1024)S(1)} %get-tuple-element.416, s32[512]{0:T(512)S(1)} %iota_add_fusion.7), kind=kOutput, calls=%fused_computation.16.clone.1 | convolution fusion | flops 1611661312 | bytes 1320964 | tf_op jit(solution)/shard_map/while/body/eval_jaxpr/dot_general | solution.py:52
  135.9 2.7 %fusion.47 = f32[16,512,128]{2,1,0:T(8,128)} fusion(f32[16,512,128]{2,1,0:T(8,128)} %get-tuple-element.409, s32[]{:T(128)S(6)} %copy.40, f32[2048,128]{1,0:T(8,128)S(1)} %get-tuple-element.418, s32[2048]{0:T(1024)S(1)} %get-tuple-element.416, s32[512]{0:T(512)S(1)} %iota_add_fusion.7), kind=kOutput, calls=%fused_computation.16.clone.1 | convolution fusion | flops 1611661312 | bytes 1320964 | tf_op jit(solution)/shard_map/while/body/eval_jaxpr/dot_general | solution.py:52
  139.8 2.7 %fusion.47 = f32[16,512,128]{2,1,0:T(8,128)} fusion(f32[16,512,128]{2,1,0:T(8,128)} %get-tuple-element.409, s32[]{:T(128)S(6)} %copy.40, f32[2048,128]{1,0:T(8,128)S(1)} %get-tuple-element.418, s32[2048]{0:T(1024)S(1)} %get-tuple-element.416, s32[512]{0:T(512)S(1)} %iota_add_fusion.7), kind=kOutput, calls=%fused_computation.16.clone.1 | convolution fusion | flops 1611661312 | bytes 1320964 | tf_op jit(solution)/shard_map/while/body/eval_jaxpr/dot_general | solution.py:52
  143.8 2.7 %fusion.47 = f32[16,512,128]{2,1,0:T(8,128)} fusion(f32[16,512,128]{2,1,0:T(8,128)} %get-tuple-element.409, s32[]{:T(128)S(6)} %copy.40, f32[2048,128]{1,0:T(8,128)S(1)} %get-tuple-element.418, s32[2048]{0:T(1024)S(1)} %get-tuple-element.416, s32[512]{0:T(512)S(1)} %iota_add_fusion.7), kind=kOutput, calls=%fused_computation.16.clone.1 | convolution fusion | flops 1611661312 | bytes 1320964 | tf_op jit(solution)/shard_map/while/body/eval_jaxpr/dot_general | solution.py:52
  147.7 2.7 %fusion.47 = f32[16,512,128]{2,1,0:T(8,128)} fusion(f32[16,512,128]{2,1,0:T(8,128)} %get-tuple-element.409, s32[]{:T(128)S(6)} %copy.40, f32[2048,128]{1,0:T(8,128)S(1)} %get-tuple-element.418, s32[2048]{0:T(1024)S(1)} %get-tuple-element.416, s32[512]{0:T(512)S(1)} %iota_add_fusion.7), kind=kOutput, calls=%fused_computation.16.clone.1 | convolution fusion | flops 1611661312 | bytes 1320964 | tf_op jit(solution)/shard_map/while/body/eval_jaxpr/dot_general | solution.py:52
  151.6 2.7 %fusion.47 = f32[16,512,128]{2,1,0:T(8,128)} fusion(f32[16,512,128]{2,1,0:T(8,128)} %get-tuple-element.409, s32[]{:T(128)S(6)} %copy.40, f32[2048,128]{1,0:T(8,128)S(1)} %get-tuple-element.418, s32[2048]{0:T(1024)S(1)} %get-tuple-element.416, s32[512]{0:T(512)S(1)} %iota_add_fusion.7), kind=kOutput, calls=%fused_computation.16.clone.1 | convolution fusion | flops 1611661312 | bytes 1320964 | tf_op jit(solution)/shard_map/while/body/eval_jaxpr/dot_general | solution.py:52
  155.5 2.7 %fusion.47 = f32[16,512,128]{2,1,0:T(8,128)} fusion(f32[16,512,128]{2,1,0:T(8,128)} %get-tuple-element.409, s32[]{:T(128)S(6)} %copy.40, f32[2048,128]{1,0:T(8,128)S(1)} %get-tuple-element.418, s32[2048]{0:T(1024)S(1)} %get-tuple-element.416, s32[512]{0:T(512)S(1)} %iota_add_fusion.7), kind=kOutput, calls=%fused_computation.16.clone.1 | convolution fusion | flops 1611661312 | bytes 1320964 | tf_op jit(solution)/shard_map/while/body/eval_jaxpr/dot_general | solution.py:52
  159.5 2.7 %fusion.47 = f32[16,512,128]{2,1,0:T(8,128)} fusion(f32[16,512,128]{2,1,0:T(8,128)} %get-tuple-element.409, s32[]{:T(128)S(6)} %copy.40, f32[2048,128]{1,0:T(8,128)S(1)} %get-tuple-element.418, s32[2048]{0:T(1024)S(1)} %get-tuple-element.416, s32[512]{0:T(512)S(1)} %iota_add_fusion.7), kind=kOutput, calls=%fused_computation.16.clone.1 | convolution fusion | flops 1611661312 | bytes 1320964 | tf_op jit(solution)/shard_map/while/body/eval_jaxpr/dot_general | solution.py:52
  162.1 3.9 %multiply_reduce_fusion = f32[]{:T(128)} fusion(f32[16,512,128]{2,1,0:T(8,128)} %get-tuple-element.131), kind=kLoop, calls=%fused_computation.27 | loop fusion | flops 2097151 | bytes 4194308 | tf_op jit(solution)/shard_map/reduce_sum | solution.py:104
  166.0 9.8 %psum.28 = f32[]{:T(128)} all-reduce(f32[]{:T(128)} %multiply_reduce_fusion), channel_id=1, replica_groups=mesh['dp_0'=4,'dp_1'=4,'dp_2'=2,'mp'=4] {'dp_0'}, use_global_device_ids=true, to_apply=%region_12.13 | all-reduce | flops 1 | bytes 8 | tf_op jit(solution)/shard_map/psum | solution.py:20
  175.8 9.5 %psum.29 = f32[]{:T(128)} all-reduce(f32[]{:T(128)} %psum.28), channel_id=1, replica_groups=mesh['dp_0'=4,'dp_1'=4,'dp_2'=2,'mp'=4] {'dp_1'}, use_global_device_ids=true, to_apply=%region_13.14 | all-reduce | flops 1 | bytes 8 | tf_op jit(solution)/shard_map/psum | solution.py:20
  185.3 3.1 %psum.30 = f32[]{:T(128)} all-reduce(f32[]{:T(128)} %psum.29), channel_id=1, replica_groups=mesh['dp_0'=4,'dp_1'=4,'dp_2'=2,'mp'=4] {'dp_2'}, use_global_device_ids=true, to_apply=%region_14.15 | all-reduce | flops 1 | bytes 8 | tf_op jit(solution)/shard_map/psum | solution.py:20
  188.4 11.1 %psum.31 = f32[]{:T(128)} all-reduce(f32[]{:T(128)} %psum.30), channel_id=1, replica_groups=mesh['dp_0'=4,'dp_1'=4,'dp_2'=2,'mp'=4] {'mp'}, use_global_device_ids=true, to_apply=%region_15.16 | all-reduce | flops 1 | bytes 8 | tf_op jit(solution)/shard_map/psum | solution.py:20
  200.3 2.7 %broadcast_multiply_fusion = f32[16,512,128]{2,1,0:T(8,128)S(1)} fusion(f32[16,512,128]{2,1,0:T(8,128)} %get-tuple-element.131, f32[]{:T(128)S(6)} %div.34), kind=kLoop, calls=%fused_computation.28 | loop fusion | flops 1048576 | bytes 8388612 | tf_op jit(solution)/shard_map/mul | solution.py:108
  203.7 1.3 copy-done.1
  205.0 7.3 %multiply_subtract_fusion = (f32[8192,128]{1,0:T(8,128)}, f32[8192,128]{1,0:T(8,128)}, f32[8192,128]{1,0:T(8,128)}) fusion(f32[8192,128]{1,0:T(8,128)S(1)} %copy-done, f32[16,512,128]{2,1,0:T(8,128)S(1)} %broadcast_multiply_fusion, f32[8192,128]{1,0:T(8,128)S(1)} %copy-done.1, f32[8192,128]{1,0:T(8,128)} %param.15), kind=kLoop, calls=%fused_computation.26 | loop fusion | flops 15728640 | bytes 29360128 | tf_op jit(solution)/shard_map/sub | solution.py:113
  (104 shorter events, 40.3 us)
Async XLA Ops:
  78.7 20.7 %all-to-all-start.1 = ((f32[32,64,128]{2,1,0:T(8,128)}), f32[32,64,128]{2,1,0:T(8,128)S(1)}, u32[]{:S(2)}, u32[]{:S(2)}) async-start(f32[32,64,128]{2,1,0:T(8,128)} %bitcast.7), calls=%async_computation.1 | async-start | bytes 2097152 | tf_op jit(solution)/shard_map/all_to_all | solution.py:97
  200.2 3.5 %copy-start = (f32[8192,128]{1,0:T(8,128)S(1)}, f32[8192,128]{1,0:T(8,128)}, u32[]{:S(2)}) copy-start(f32[8192,128]{1,0:T(8,128)} %param.13) | copy-start | bytes 12582916
  200.2 4.7 %copy-start.1 = (f32[8192,128]{1,0:T(8,128)S(1)}, f32[8192,128]{1,0:T(8,128)}, u32[]{:S(2)}) copy-start(f32[8192,128]{1,0:T(8,128)} %param.14) | copy-start | bytes 12582916
where the time goes:
time: 214 us; the launch traced here: 212 us
  matrix products  53 us (25%)
  blocking collectives  49.1 us (23%)
  other arithmetic  48.4 us (23%)
  local copies, waits for them, and re-layouts  25.9 us (12%)
  waiting for transfers between devices  16.6 us (8%)
  loops' own time  13.8 us (6%)
  starting transfers between devices  3.93 us (2%)
    dot_general x16, matrix products, gather_one_block(): jnp.dot(match.astype(jnp.float32), got, precision=lax.Precision.HIGHEST,...  43 us
    psum x4, blocking collectives, by_axis(): shard = lax.psum(shard, axis)  33.5 us
    all_to_all x1, waiting for transfers between devices, body(): lax.all_to_all(sums.reshape(peers, room, width), DP, split_axis=0, concat...  16.6 us
    all_to_all x1, blocking collectives, body(): lax.all_to_all(row_marks, DP, split_axis=0, concat_axis=0, tiled=True)  15.6 us
    add x16, other arithmetic, gather_one_block(): target = start + jnp.arange(step, dtype=jnp.int32)  10.3 us
    dot_general x4, matrix products, pack_one_block(): jnp.dot(match.astype(jnp.bfloat16), values, preferred_element_type=jnp.fl...  10 us
    dynamic_slice x16, local copies, waits for them, and re-layouts, gather_rows(): lax.map(gather_one_block, block_starts(rows_dev, step))  9.31 us
    reduce_or x4, other arithmetic, first_block(): return jnp.logical_not(jnp.any(earlier, axis=1))  7.6 us
  transfers between devices with their start and end apart: 1, of which 1 were waited for; matrix products, arithmetic and copies ran while one was open for 0% of the time, Pallas kernels for 0%

commit v1 on v0

--- a/solution.py
+++ b/solution.py
@@ -17,7 +17,8 @@
 
 def by_axis(shard, axes):
     for axis in axes:
-        shard = lax.psum(shard, axis)
+        parts = lax.all_gather(shard, axis)
+        shard = jnp.sum(parts, axis=0)
     return shard
 
 

time: 214 us -> 221 us (1.033)
  local copies, waits for them, and re-layouts: 25.9 us -> 34 us
  blocking collectives: 49.1 us -> 46.6 us
  other arithmetic: 48.4 us -> 50.8 us
    psum x4 -> x0, blocking collectives: 33.5 us -> none  [by_axis(): shard = lax.psum(shard, axis)]
    unnamed x0 -> x4, blocking collectives: none -> 30.9 us
    unnamed x5 -> x25, local copies, waits for them, and re-layouts: 1.99 us -> 10.1 us
    reduce_sum x0 -> x4, other arithmetic: none -> 2.41 us  [by_axis(): shard = jnp.sum(parts, axis=0)]
where the time goes in v1:
time: 221 us; the launch traced here: 220 us
  matrix products  53 us (24%)
  other arithmetic  50.8 us (23%)
  blocking collectives  46.6 us (21%)
  local copies, waits for them, and re-layouts  34 us (15%)
  waiting for transfers between devices  15.9 us (7%)
  loops' own time  13.8 us (6%)
  starting transfers between devices  3.93 us (2%)
    dot_general x16, matrix products, gather_one_block(): jnp.dot(match.astype(jnp.float32), got, precision=lax.Precision.HIGHEST,...  43 us
    unnamed x4, blocking collectives  30.9 us
    all_to_all x1, waiting for transfers between devices, body(): lax.all_to_all(sums.reshape(peers, room, width), DP, split_axis=0, concat...  15.9 us
    all_to_all x1, blocking collectives, body(): lax.all_to_all(row_marks, DP, split_axis=0, concat_axis=0, tiled=True)  15.6 us
    add x16, other arithmetic, gather_one_block(): target = start + jnp.arange(step, dtype=jnp.int32)  10.3 us
    unnamed x25, local copies, waits for them, and re-layouts  10.1 us
    dot_general x4, matrix products, pack_one_block(): jnp.dot(match.astype(jnp.bfloat16), values, preferred_element_type=jnp.fl...  10 us
    dynamic_slice x16, local copies, waits for them, and re-layouts, gather_rows(): lax.map(gather_one_block, block_starts(rows_dev, step))  9.31 us
  transfers between devices with their start and end apart: 1, of which 1 were waited for; matrix products, arithmetic and copies ran while one was open for 0% of the time, Pallas kernels for 0%

profile of v1, /device:TPU:0, one launch (start us, length us, event | category | flops | bytes accessed | tf_op | source)
XLA Modules:
  0.0 219.6 jit_solution(15470682601935831258)
XLA Ops:
  1.4 22.3 %while.46 = (s32[]{:T(128)}, pred[4,512]{1,0:T(4,128)(4,1)S(1)}, s32[2048]{0:T(1024)}, s32[4]{0:T(128)S(1)}, s32[]{:T(128)}, /*index=5*/s32[]{:T(128)}, s32[]{:T(128)}) while((s32[]{:T(128)}, pred[4,512]{1,0:T(4,128)(4,1)S(1)}, s32[2048]{0:T(1024)}, s32[4]{0:T(128)S(1)}, s32[]{:T(128)}, /*index=5*/s32[]{:T(128)}, s32[]{:T(128)}) %tuple.67), condition=%wide.region_2.3_spmd.clone, body=%wide.region_0.2_spmd.clone.sunk | while | flops 4194821 | bytes 22159 | solution.py:80
  4.2 0.8 dynamic_slice.38
  5.0 1.9 fusion.48
  10.6 1.9 fusion.48
  16.1 1.9 fusion.48
  21.7 1.9 fusion.48
  23.7 20.1 %while.43 = (s32[]{:T(128)}, s32[4,512]{1,0:T(4,128)S(1)}, pred[4,512]{1,0:T(4,128)(4,1)S(1)}, s32[2048]{0:T(1024)S(1)}, s32[4]{0:T(128)S(1)}, /*index=5*/s32[2048]{0:T(1024)}, s32[]{:T(128)}, s32[]{:T(128)}, s32[]{:T(128)}) while((s32[]{:T(128)}, s32[4,512]{1,0:T(4,128)S(1)}, pred[4,512]{1,0:T(4,128)(4,1)S(1)}, s32[2048]{0:T(1024)S(1)}, ...), condition=%wide.region_5.6_spmd, body=%wide.region_3.5_spmd.sunk | while | flops 6290949 | bytes 41119 | solution.py:92
  26.8 1.8 convert_reduce_fusion.3
  31.9 1.8 convert_reduce_fusion.3
  36.9 1.8 convert_reduce_fusion.3
  41.9 1.8 convert_reduce_fusion.3
  44.5 18.4 %while.44 = (s32[]{:T(128)}, f32[4,512,128]{2,1,0:T(8,128)}, s32[4,512]{1,0:T(4,128)S(1)}, s32[2048]{0:T(1024)S(1)}, s32[4]{0:T(128)S(1)}, /*index=5*/bf16[2048,...) while((s32[]{:T(128)}, f32[4,512,128]{2,1,0:T(8,128)}, s32[4,512]{1,0:T(4,128)S(1)}, ...), condition=%wide.region_8.9_spmd, body=%wide.region_6.8_spmd.sunk | while | flops 272629760 | bytes 823421 | solution.py:43
  46.6 2.5 %fusion.43 = f32[4,512,128]{2,1,0:T(8,128)} fusion(f32[4,512,128]{2,1,0:T(8,128)} %get-tuple-element.385, s32[]{:T(128)S(6)} %copy.32, bf16[2048,128]{1,0:T(8,128)(2,1)} %get-tuple-element.398, s32[2048]{0:T(1024)S(1)} %get-tuple-element.396, s32[512]{0:T(512)S(1)} %iota_add_fusion.6), kind=kOutput, calls=%fused_computation.9.clone.1 | convolution fusion | flops 269484032 | bytes 796676 | tf_op jit(solution)/shard_map/while/body/eval_jaxpr/dot_general | solution.py:39
  51.2 2.5 %fusion.43 = f32[4,512,128]{2,1,0:T(8,128)} fusion(f32[4,512,128]{2,1,0:T(8,128)} %get-tuple-element.385, s32[]{:T(128)S(6)} %copy.32, bf16[2048,128]{1,0:T(8,128)(2,1)} %get-tuple-element.398, s32[2048]{0:T(1024)S(1)} %get-tuple-element.396, s32[512]{0:T(512)S(1)} %iota_add_fusion.6), kind=kOutput, calls=%fused_computation.9.clone.1 | convolution fusion | flops 269484032 | bytes 796676 | tf_op jit(solution)/shard_map/while/body/eval_jaxpr/dot_general | solution.py:39
  55.8 2.5 %fusion.43 = f32[4,512,128]{2,1,0:T(8,128)} fusion(f32[4,512,128]{2,1,0:T(8,128)} %get-tuple-element.385, s32[]{:T(128)S(6)} %copy.32, bf16[2048,128]{1,0:T(8,128)(2,1)} %get-tuple-element.398, s32[2048]{0:T(1024)S(1)} %get-tuple-element.396, s32[512]{0:T(512)S(1)} %iota_add_fusion.6), kind=kOutput, calls=%fused_computation.9.clone.1 | convolution fusion | flops 269484032 | bytes 796676 | tf_op jit(solution)/shard_map/while/body/eval_jaxpr/dot_general | solution.py:39
  60.4 2.5 %fusion.43 = f32[4,512,128]{2,1,0:T(8,128)} fusion(f32[4,512,128]{2,1,0:T(8,128)} %get-tuple-element.385, s32[]{:T(128)S(6)} %copy.32, bf16[2048,128]{1,0:T(8,128)(2,1)} %get-tuple-element.398, s32[2048]{0:T(1024)S(1)} %get-tuple-element.396, s32[512]{0:T(512)S(1)} %iota_add_fusion.6), kind=kOutput, calls=%fused_computation.9.clone.1 | convolution fusion | flops 269484032 | bytes 796676 | tf_op jit(solution)/shard_map/while/body/eval_jaxpr/dot_general | solution.py:39
  63.1 15.6 %all_to_all.11 = f32[32,1,64]{2,1,0:T(1,128)S(1)} all-to-all(f32[32,1,64]{2,1,0:T(1,128)S(1)} %convert_element_type.26), channel_id=1, replica_groups=mesh['dp_0'=4,'dp_1'=4,'dp_2'=2,'mp'=4] {'dp_0','dp_1','dp_2'}, dimensions={0} | all-to-all | bytes 16384 | tf_op jit(solution)/shard_map/all_to_all | solution.py:101
  78.7 3.9 %all-to-all-start.1 = ((f32[32,64,128]{2,1,0:T(8,128)}), f32[32,64,128]{2,1,0:T(8,128)S(1)}, u32[]{:S(2)}, u32[]{:S(2)}) async-start(f32[32,64,128]{2,1,0:T(8,128)} %bitcast.7), calls=%async_computation.1 | async-start | bytes 2097152 | tf_op jit(solution)/shard_map/all_to_all | solution.py:98
  83.5 15.9 %all-to-all-done.1 = f32[32,64,128]{2,1,0:T(8,128)S(1)} async-done(((f32[32,64,128]{2,1,0:T(8,128)}), f32[32,64,128]{2,1,0:T(8,128)S(1)}, u32[]{:S(2)}, u32[]{:S(2)}) %all-to-all-start.1) | async-done | bytes 1048608 | tf_op jit(solution)/shard_map/all_to_all | solution.py:98
  99.4 62.8 %while.45 = (s32[]{:T(128)}, f32[16,512,128]{2,1,0:T(8,128)}, s32[2048]{0:T(1024)S(1)}, s32[16]{0:T(128)S(1)}, f32[2048,128]{1,0:T(8,128)S(1)}, /*index=5*/s32[]{:T(128)}) while((s32[]{:T(128)}, f32[16,512,128]{2,1,0:T(8,128)}, s32[2048]{0:T(1024)S(1)}, s32[16]{0:T(128)S(1)}, f32[2048,128]{1,0:T(8,128)S(1)}, /*index=5*/s32[]{:T(128)}) %tuple.79), condition=%wide.region_10.11_spmd, body=%wide.region_9.10_spmd.sunk | while | flops 1611661824 | bytes 1323105 | solution.py:60
  100.6 2.7 %fusion.47 = f32[16,512,128]{2,1,0:T(8,128)} fusion(f32[16,512,128]{2,1,0:T(8,128)} %get-tuple-element.409, s32[]{:T(128)S(6)} %copy.40, f32[2048,128]{1,0:T(8,128)S(1)} %get-tuple-element.418, s32[2048]{0:T(1024)S(1)} %get-tuple-element.416, s32[512]{0:T(512)S(1)} %iota_add_fusion.7), kind=kOutput, calls=%fused_computation.16.clone.1 | convolution fusion | flops 1611661312 | bytes 1320964 | tf_op jit(solution)/shard_map/while/body/eval_jaxpr/dot_general | solution.py:53
  104.6 2.7 %fusion.47 = f32[16,512,128]{2,1,0:T(8,128)} fusion(f32[16,512,128]{2,1,0:T(8,128)} %get-tuple-element.409, s32[]{:T(128)S(6)} %copy.40, f32[2048,128]{1,0:T(8,128)S(1)} %get-tuple-element.418, s32[2048]{0:T(1024)S(1)} %get-tuple-element.416, s32[512]{0:T(512)S(1)} %iota_add_fusion.7), kind=kOutput, calls=%fused_computation.16.clone.1 | convolution fusion | flops 1611661312 | bytes 1320964 | tf_op jit(solution)/shard_map/while/body/eval_jaxpr/dot_general | solution.py:53
  108.5 2.7 %fusion.47 = f32[16,512,128]{2,1,0:T(8,128)} fusion(f32[16,512,128]{2,1,0:T(8,128)} %get-tuple-element.409, s32[]{:T(128)S(6)} %copy.40, f32[2048,128]{1,0:T(8,128)S(1)} %get-tuple-element.418, s32[2048]{0:T(1024)S(1)} %get-tuple-element.416, s32[512]{0:T(512)S(1)} %iota_add_fusion.7), kind=kOutput, calls=%fused_computation.16.clone.1 | convolution fusion | flops 1611661312 | bytes 1320964 | tf_op jit(solution)/shard_map/while/body/eval_jaxpr/dot_general | solution.py:53
  112.4 2.7 %fusion.47 = f32[16,512,128]{2,1,0:T(8,128)} fusion(f32[16,512,128]{2,1,0:T(8,128)} %get-tuple-element.409, s32[]{:T(128)S(6)} %copy.40, f32[2048,128]{1,0:T(8,128)S(1)} %get-tuple-element.418, s32[2048]{0:T(1024)S(1)} %get-tuple-element.416, s32[512]{0:T(512)S(1)} %iota_add_fusion.7), kind=kOutput, calls=%fused_computation.16.clone.1 | convolution fusion | flops 1611661312 | bytes 1320964 | tf_op jit(solution)/shard_map/while/body/eval_jaxpr/dot_general | solution.py:53
  116.3 2.7 %fusion.47 = f32[16,512,128]{2,1,0:T(8,128)} fusion(f32[16,512,128]{2,1,0:T(8,128)} %get-tuple-element.409, s32[]{:T(128)S(6)} %copy.40, f32[2048,128]{1,0:T(8,128)S(1)} %get-tuple-element.418, s32[2048]{0:T(1024)S(1)} %get-tuple-element.416, s32[512]{0:T(512)S(1)} %iota_add_fusion.7), kind=kOutput, calls=%fused_computation.16.clone.1 | convolution fusion | flops 1611661312 | bytes 1320964 | tf_op jit(solution)/shard_map/while/body/eval_jaxpr/dot_general | solution.py:53
  120.2 2.7 %fusion.47 = f32[16,512,128]{2,1,0:T(8,128)} fusion(f32[16,512,128]{2,1,0:T(8,128)} %get-tuple-element.409, s32[]{:T(128)S(6)} %copy.40, f32[2048,128]{1,0:T(8,128)S(1)} %get-tuple-element.418, s32[2048]{0:T(1024)S(1)} %get-tuple-element.416, s32[512]{0:T(512)S(1)} %iota_add_fusion.7), kind=kOutput, calls=%fused_computation.16.clone.1 | convolution fusion | flops 1611661312 | bytes 1320964 | tf_op jit(solution)/shard_map/while/body/eval_jaxpr/dot_general | solution.py:53
  124.2 2.7 %fusion.47 = f32[16,512,128]{2,1,0:T(8,128)} fusion(f32[16,512,128]{2,1,0:T(8,128)} %get-tuple-element.409, s32[]{:T(128)S(6)} %copy.40, f32[2048,128]{1,0:T(8,128)S(1)} %get-tuple-element.418, s32[2048]{0:T(1024)S(1)} %get-tuple-element.416, s32[512]{0:T(512)S(1)} %iota_add_fusion.7), kind=kOutput, calls=%fused_computation.16.clone.1 | convolution fusion | flops 1611661312 | bytes 1320964 | tf_op jit(solution)/shard_map/while/body/eval_jaxpr/dot_general | solution.py:53
  128.1 2.7 %fusion.47 = f32[16,512,128]{2,1,0:T(8,128)} fusion(f32[16,512,128]{2,1,0:T(8,128)} %get-tuple-element.409, s32[]{:T(128)S(6)} %copy.40, f32[2048,128]{1,0:T(8,128)S(1)} %get-tuple-element.418, s32[2048]{0:T(1024)S(1)} %get-tuple-element.416, s32[512]{0:T(512)S(1)} %iota_add_fusion.7), kind=kOutput, calls=%fused_computation.16.clone.1 | convolution fusion | flops 1611661312 | bytes 1320964 | tf_op jit(solution)/shard_map/while/body/eval_jaxpr/dot_general | solution.py:53
  132.0 2.7 %fusion.47 = f32[16,512,128]{2,1,0:T(8,128)} fusion(f32[16,512,128]{2,1,0:T(8,128)} %get-tuple-element.409, s32[]{:T(128)S(6)} %copy.40, f32[2048,128]{1,0:T(8,128)S(1)} %get-tuple-element.418, s32[2048]{0:T(1024)S(1)} %get-tuple-element.416, s32[512]{0:T(512)S(1)} %iota_add_fusion.7), kind=kOutput, calls=%fused_computation.16.clone.1 | convolution fusion | flops 1611661312 | bytes 1320964 | tf_op jit(solution)/shard_map/while/body/eval_jaxpr/dot_general | solution.py:53
  135.9 2.7 %fusion.47 = f32[16,512,128]{2,1,0:T(8,128)} fusion(f32[16,512,128]{2,1,0:T(8,128)} %get-tuple-element.409, s32[]{:T(128)S(6)} %copy.40, f32[2048,128]{1,0:T(8,128)S(1)} %get-tuple-element.418, s32[2048]{0:T(1024)S(1)} %get-tuple-element.416, s32[512]{0:T(512)S(1)} %iota_add_fusion.7), kind=kOutput, calls=%fused_computation.16.clone.1 | convolution fusion | flops 1611661312 | bytes 1320964 | tf_op jit(solution)/shard_map/while/body/eval_jaxpr/dot_general | solution.py:53
  139.9 2.7 %fusion.47 = f32[16,512,128]{2,1,0:T(8,128)} fusion(f32[16,512,128]{2,1,0:T(8,128)} %get-tuple-element.409, s32[]{:T(128)S(6)} %copy.40, f32[2048,128]{1,0:T(8,128)S(1)} %get-tuple-element.418, s32[2048]{0:T(1024)S(1)} %get-tuple-element.416, s32[512]{0:T(512)S(1)} %iota_add_fusion.7), kind=kOutput, calls=%fused_computation.16.clone.1 | convolution fusion | flops 1611661312 | bytes 1320964 | tf_op jit(solution)/shard_map/while/body/eval_jaxpr/dot_general | solution.py:53
  143.8 2.7 %fusion.47 = f32[16,512,128]{2,1,0:T(8,128)} fusion(f32[16,512,128]{2,1,0:T(8,128)} %get-tuple-element.409, s32[]{:T(128)S(6)} %copy.40, f32[2048,128]{1,0:T(8,128)S(1)} %get-tuple-element.418, s32[2048]{0:T(1024)S(1)} %get-tuple-element.416, s32[512]{0:T(512)S(1)} %iota_add_fusion.7), kind=kOutput, calls=%fused_computation.16.clone.1 | convolution fusion | flops 1611661312 | bytes 1320964 | tf_op jit(solution)/shard_map/while/body/eval_jaxpr/dot_general | solution.py:53
  147.7 2.7 %fusion.47 = f32[16,512,128]{2,1,0:T(8,128)} fusion(f32[16,512,128]{2,1,0:T(8,128)} %get-tuple-element.409, s32[]{:T(128)S(6)} %copy.40, f32[2048,128]{1,0:T(8,128)S(1)} %get-tuple-element.418, s32[2048]{0:T(1024)S(1)} %get-tuple-element.416, s32[512]{0:T(512)S(1)} %iota_add_fusion.7), kind=kOutput, calls=%fused_computation.16.clone.1 | convolution fusion | flops 1611661312 | bytes 1320964 | tf_op jit(solution)/shard_map/while/body/eval_jaxpr/dot_general | solution.py:53
  151.6 2.7 %fusion.47 = f32[16,512,128]{2,1,0:T(8,128)} fusion(f32[16,512,128]{2,1,0:T(8,128)} %get-tuple-element.409, s32[]{:T(128)S(6)} %copy.40, f32[2048,128]{1,0:T(8,128)S(1)} %get-tuple-element.418, s32[2048]{0:T(1024)S(1)} %get-tuple-element.416, s32[512]{0:T(512)S(1)} %iota_add_fusion.7), kind=kOutput, calls=%fused_computation.16.clone.1 | convolution fusion | flops 1611661312 | bytes 1320964 | tf_op jit(solution)/shard_map/while/body/eval_jaxpr/dot_general | solution.py:53
  155.5 2.7 %fusion.47 = f32[16,512,128]{2,1,0:T(8,128)} fusion(f32[16,512,128]{2,1,0:T(8,128)} %get-tuple-element.409, s32[]{:T(128)S(6)} %copy.40, f32[2048,128]{1,0:T(8,128)S(1)} %get-tuple-element.418, s32[2048]{0:T(1024)S(1)} %get-tuple-element.416, s32[512]{0:T(512)S(1)} %iota_add_fusion.7), kind=kOutput, calls=%fused_computation.16.clone.1 | convolution fusion | flops 1611661312 | bytes 1320964 | tf_op jit(solution)/shard_map/while/body/eval_jaxpr/dot_general | solution.py:53
  159.5 2.7 %fusion.47 = f32[16,512,128]{2,1,0:T(8,128)} fusion(f32[16,512,128]{2,1,0:T(8,128)} %get-tuple-element.409, s32[]{:T(128)S(6)} %copy.40, f32[2048,128]{1,0:T(8,128)S(1)} %get-tuple-element.418, s32[2048]{0:T(1024)S(1)} %get-tuple-element.416, s32[512]{0:T(512)S(1)} %iota_add_fusion.7), kind=kOutput, calls=%fused_computation.16.clone.1 | convolution fusion | flops 1611661312 | bytes 1320964 | tf_op jit(solution)/shard_map/while/body/eval_jaxpr/dot_general | solution.py:53
  162.2 3.9 %multiply_reduce_fusion = f32[]{:T(128)} fusion(f32[16,512,128]{2,1,0:T(8,128)} %get-tuple-element.131), kind=kLoop, calls=%fused_computation.27 | loop fusion | flops 2097151 | bytes 4194308 | tf_op jit(solution)/shard_map/reduce_sum | solution.py:105
  166.1 1.4 dynamic-update-slice
  168.1 9.2 %all-reduce = f32[4]{0:T(128)S(1)} all-reduce(f32[4]{0:T(128)S(1)} %dynamic-update-slice), channel_id=1, replica_groups=mesh['dp_0'=4,'dp_1'=4,'dp_2'=2,'mp'=4] {'dp_0'}, use_global_device_ids=true, to_apply=%add | all-reduce | flops 4 | bytes 32
  177.9 1.4 dynamic-update-slice.1
  179.9 8.9 %all-reduce.1 = f32[4]{0:T(128)S(1)} all-reduce(f32[4]{0:T(128)S(1)} %dynamic-update-slice.1), channel_id=1, replica_groups=mesh['dp_0'=4,'dp_1'=4,'dp_2'=2,'mp'=4] {'dp_1'}, use_global_device_ids=true, to_apply=%add.1 | all-reduce | flops 4 | bytes 32
  189.4 1.4 dynamic-update-slice.2
  191.3 2.4 %all-reduce.2 = f32[2]{0:T(128)S(1)} all-reduce(f32[2]{0:T(128)S(1)} %dynamic-update-slice.2), channel_id=1, replica_groups=mesh['dp_0'=4,'dp_1'=4,'dp_2'=2,'mp'=4] {'dp_2'}, use_global_device_ids=true, to_apply=%add.2 | all-reduce | flops 2 | bytes 16
  194.4 1.4 dynamic-update-slice.3
  195.8 10.5 %all-reduce.3 = f32[4]{0:T(128)S(1)} all-reduce(f32[4]{0:T(128)S(1)} %dynamic-update-slice.3), channel_id=1, replica_groups=mesh['dp_0'=4,'dp_1'=4,'dp_2'=2,'mp'=4] {'mp'}, use_global_device_ids=true, to_apply=%add.3 | all-reduce | flops 4 | bytes 32
  207.6 2.7 %broadcast_multiply_fusion = f32[16,512,128]{2,1,0:T(8,128)S(1)} fusion(f32[16,512,128]{2,1,0:T(8,128)} %get-tuple-element.131, f32[]{:T(128)S(6)} %div.34), kind=kLoop, calls=%fused_computation.28 | loop fusion | flops 1048576 | bytes 8388612 | tf_op jit(solution)/shard_map/mul | solution.py:109
  211.0 1.3 copy-done.1
  212.3 7.3 %multiply_subtract_fusion = (f32[8192,128]{1,0:T(8,128)}, f32[8192,128]{1,0:T(8,128)}, f32[8192,128]{1,0:T(8,128)}) fusion(f32[8192,128]{1,0:T(8,128)S(1)} %copy-done, f32[16,512,128]{2,1,0:T(8,128)S(1)} %broadcast_multiply_fusion, f32[8192,128]{1,0:T(8,128)S(1)} %copy-done.1, f32[8192,128]{1,0:T(8,128)} %param.15), kind=kLoop, calls=%fused_computation.26 | loop fusion | flops 15728640 | bytes 29360128 | tf_op jit(solution)/shard_map/sub | solution.py:114
  (128 shorter events, 48.3 us)
Async XLA Ops:
  44.5 38.1 %copy-start.5 = (u32[128]{0:T(128)S(1)}, u32[128]{0:T(128)}, u32[]{:S(2)}) copy-start(u32[128]{0:T(128)} %constant.94) | copy-start | bytes 1540
  78.7 20.7 %all-to-all-start.1 = ((f32[32,64,128]{2,1,0:T(8,128)}), f32[32,64,128]{2,1,0:T(8,128)S(1)}, u32[]{:S(2)}, u32[]{:S(2)}) async-start(f32[32,64,128]{2,1,0:T(8,128)} %bitcast.7), calls=%async_computation.1 | async-start | bytes 2097152 | tf_op jit(solution)/shard_map/all_to_all | solution.py:98
  162.2 5.4 %copy-start.4 = (u32[128]{0:T(128)S(1)}, u32[128]{0:T(128)}, u32[]{:S(2)}) copy-start(u32[128]{0:T(128)} %constant.99) | copy-start | bytes 1540
  162.2 17.1 %copy-start.3 = (u32[128]{0:T(128)S(1)}, u32[128]{0:T(128)}, u32[]{:S(2)}) copy-start(u32[128]{0:T(128)} %constant.104) | copy-start | bytes 1540
  162.2 28.6 %copy-start.2 = (u32[128]{0:T(128)S(1)}, u32[128]{0:T(128)}, u32[]{:S(2)}) copy-start(u32[128]{0:T(128)} %constant.109) | copy-start | bytes 1540
  207.6 3.5 %copy-start = (f32[8192,128]{1,0:T(8,128)S(1)}, f32[8192,128]{1,0:T(8,128)}, u32[]{:S(2)}) copy-start(f32[8192,128]{1,0:T(8,128)} %param.13) | copy-start | bytes 12582916
  207.6 4.7 %copy-start.1 = (f32[8192,128]{1,0:T(8,128)S(1)}, f32[8192,128]{1,0:T(8,128)}, u32[]{:S(2)}) copy-start(f32[8192,128]{1,0:T(8,128)} %param.14) | copy-start | bytes 12582916
